TPU v7x, 32 devices: a whole 2x2x4 slice. The times are simulated.
32 devices in a mesh: gx: 8 (over y, x, core), gy: 4 (over z).
Axes of the slice: x: 2, y: 2, z: 4, core: 2. Of those that a mesh axis runs over, the one named last changes fastest.
Arguments:
- terminal: float32 [128, 2048], P('gx', 'gy'), may hold values from -15 to 15
- initial_density: float32 [128, 2048], P('gx', 'gy'), may hold values from 0.1 to 1
- density_guess: float32 [2, 128, 2048], P(None, 'gx', 'gy'), may hold values from 0.1 to 1
- diagonal: float32 [128, 2048], P('gx', 'gy'), may hold values from 0.1 to 2
Outputs:
- value_field: float32 [128, 2048], P('gx', 'gy')
- density_field: float32 [128, 2048], P('gx', 'gy')
All inputs are finite; a program needn't handle non-finite values.
Results may differ from a plain program's by a relative error of at most 0.00011.
Values sent between devices are 32-bit elements; how exact they have to be, the bound alone decides.
A program may use at most 64 MiB of HBM per device.

v0:
```python
import jax
import jax.numpy as jnp
from jax import lax
from jax.sharding import PartitionSpec as P

LEVELS = 2
STEPS = 3
inv_step = 0.5
coupling = 0.5


def padded_2(cells, sides, width):
    for axis, dim in sides:
        count = lax.axis_size(axis)
        ends = count - 1
        head = lax.slice_in_dim(cells, 0, width, axis=dim)
        tail = lax.slice_in_dim(cells, cells.shape[dim] - width, cells.shape[dim], axis=dim)
        cells = jnp.concatenate(
            [
                lax.ppermute(tail, axis, [(i, (i + 1) % count) for i in range(ends)]),
                cells,
                lax.ppermute(head, axis, [((i + 1) % count, i) for i in range(ends)]),
            ],
            axis=dim,
        )
    return cells


def apply_padded(padded, center, diagonal):
    beside = padded[2:, 1:-1] + padded[:-2, 1:-1] + padded[1:-1, 2:] + padded[1:-1, :-2]
    return (inv_step + diagonal) * center + (4.0 * center - beside)


def hamiltonian(padded):
    center = padded[1:-1, 1:-1]
    back_x = center - padded[:-2, 1:-1]
    ahead_x = padded[2:, 1:-1] - center
    back_y = center - padded[1:-1, :-2]
    ahead_y = padded[1:-1, 2:] - center
    return 0.5 * (
        jnp.maximum(back_x, 0.0) ** 2
        + jnp.minimum(ahead_x, 0.0) ** 2
        + jnp.maximum(back_y, 0.0) ** 2
        + jnp.minimum(ahead_y, 0.0) ** 2
    )


def divergence(pad_m, pad_u):
    m_mid = pad_m[1:-1, 1:-1]
    u_mid = pad_u[1:-1, 1:-1]
    speed_ahead = -(pad_u[2:, 1:-1] - u_mid)
    speed_back = -(u_mid - pad_u[:-2, 1:-1])
    flux_ahead = (
        jnp.maximum(speed_ahead, 0.0) * m_mid + jnp.minimum(speed_ahead, 0.0) * pad_m[2:, 1:-1]
    )
    flux_back = (
        jnp.maximum(speed_back, 0.0) * pad_m[:-2, 1:-1] + jnp.minimum(speed_back, 0.0) * m_mid
    )
    total = flux_ahead - flux_back
    speed_ahead = -(pad_u[1:-1, 2:] - u_mid)
    speed_back = -(u_mid - pad_u[1:-1, :-2])
    flux_ahead = (
        jnp.maximum(speed_ahead, 0.0) * m_mid + jnp.minimum(speed_ahead, 0.0) * pad_m[1:-1, 2:]
    )
    flux_back = (
        jnp.maximum(speed_back, 0.0) * pad_m[1:-1, :-2] + jnp.minimum(speed_back, 0.0) * m_mid
    )
    return total + flux_ahead - flux_back


def stencil(field, diagonal):
    padded = padded_2(field, (("gx", 0), ("gy", 1)), 1)
    return apply_padded(padded, field, diagonal)


def paired(resid, image):
    return lax.psum((jnp.sum(resid * resid), jnp.sum(resid * image)), ("gx", "gy"))


def solve(rhs, diagonal):
    answer = jnp.zeros_like(rhs)
    resid = rhs
    image = stencil(resid, diagonal)
    norm_now, product = paired(resid, image)
    alpha = norm_now / product
    direction = resid
    along = image
    for step in range(STEPS):
        answer = answer + alpha * direction
        if step + 1 < STEPS:
            resid = resid - alpha * along
            image = stencil(resid, diagonal)
            norm_next, product = paired(resid, image)
            ratio = norm_next / norm_now
            alpha = norm_next / (product - ratio * norm_next / alpha)
            direction = resid + ratio * direction
            along = image + ratio * along
            norm_now = norm_next
    return answer


def shards(terminal, initial_density, density_guess, diagonal):
    levels = [None] * LEVELS
    kept = [None] * (LEVELS + 1)
    later = terminal
    for level in reversed(range(LEVELS)):
        padded = padded_2(later, (("gx", 0), ("gy", 1)), 1)
        kept[level + 1] = padded
        rhs = inv_step * later - hamiltonian(padded) + coupling * density_guess[level]
        later = solve(rhs, diagonal)
        levels[level] = later
    density = initial_density
    for level in range(LEVELS):
        both = padded_2(jnp.stack([density, levels[level]]), (("gx", 1), ("gy", 2)), 1)
        pad_m = both[0]
        pad_u = both[1]
        rhs = inv_step * density - divergence(pad_m, pad_u)
        density = solve(rhs, diagonal)
    return (levels[0], density)


def solution(mesh):
    placed = (P("gx", "gy"), P("gx", "gy"), P(None, "gx", "gy"), P("gx", "gy"))
    return jax.shard_map(
        shards,
        mesh=mesh,
        in_specs=placed,
        out_specs=(P("gx", "gy"), P("gx", "gy")),
        check_vma=False,
    )
```

profile of v0, /device:TPU:0, one launch (start us, length us, event | category | flops | bytes accessed | tf_op | source)
XLA Modules:
  0.0 794.6 jit_solution(6539389510848766580)
XLA Ops:
  27.9 4.5 collective-permute-start.7
  34.6 42.7 %all-reduce.11 = (f32[]{:T(128)}, f32[]{:T(128)}) all-reduce(f32[]{:T(128)} %get-tuple-element.25, f32[]{:T(128)} %get-tuple-element.24), channel_id=1, replica_groups=mesh['gx'=8,'gy'=4] {'gx','gy'}, use_global_device_ids=true, to_apply=%region_1.0 | all-reduce | flops 2 | bytes 16 | tf_op jit(solution)/shard_map/psum | solution.py:77
  86.9 4.5 collective-permute-start.11
  93.6 42.6 %all-reduce.10 = (f32[]{:T(128)}, f32[]{:T(128)}) all-reduce(f32[]{:T(128)} %get-tuple-element.23, f32[]{:T(128)} %get-tuple-element.22), channel_id=1, replica_groups=mesh['gx'=8,'gy'=4] {'gx','gy'}, use_global_device_ids=true, to_apply=%region_5.0 | all-reduce | flops 2 | bytes 16 | tf_op jit(solution)/shard_map/psum | solution.py:77
  149.1 4.5 collective-permute-start.15
  155.8 41.8 %all-reduce.9 = (f32[]{:T(128)}, f32[]{:T(128)}) all-reduce(f32[]{:T(128)} %get-tuple-element.21, f32[]{:T(128)} %get-tuple-element.20), channel_id=1, replica_groups=mesh['gx'=8,'gy'=4] {'gx','gy'}, use_global_device_ids=true, to_apply=%region_9.0 | all-reduce | flops 2 | bytes 16 | tf_op jit(solution)/shard_map/psum | solution.py:77
  225.6 4.5 collective-permute-start.23
  232.2 42.6 %all-reduce.8 = (f32[]{:T(128)}, f32[]{:T(128)}) all-reduce(f32[]{:T(128)} %get-tuple-element.19, f32[]{:T(128)} %get-tuple-element.18), channel_id=1, replica_groups=mesh['gx'=8,'gy'=4] {'gx','gy'}, use_global_device_ids=true, to_apply=%region_13.0 | all-reduce | flops 2 | bytes 16 | tf_op jit(solution)/shard_map/psum | solution.py:77
  284.4 4.5 collective-permute-start.27
  291.2 42.5 %all-reduce.7 = (f32[]{:T(128)}, f32[]{:T(128)}) all-reduce(f32[]{:T(128)} %get-tuple-element.17, f32[]{:T(128)} %get-tuple-element.16), channel_id=1, replica_groups=mesh['gx'=8,'gy'=4] {'gx','gy'}, use_global_device_ids=true, to_apply=%region_17.0 | all-reduce | flops 2 | bytes 16 | tf_op jit(solution)/shard_map/psum | solution.py:77
  346.5 4.5 collective-permute-start.31
  353.2 41.9 %all-reduce.6 = (f32[]{:T(128)}, f32[]{:T(128)}) all-reduce(f32[]{:T(128)} %get-tuple-element.15, f32[]{:T(128)} %get-tuple-element.14), channel_id=1, replica_groups=mesh['gx'=8,'gy'=4] {'gx','gy'}, use_global_device_ids=true, to_apply=%region_21.0 | all-reduce | flops 2 | bytes 16 | tf_op jit(solution)/shard_map/psum | solution.py:77
  423.4 4.5 collective-permute-start.39
  430.0 42.7 %all-reduce.5 = (f32[]{:T(128)}, f32[]{:T(128)}) all-reduce(f32[]{:T(128)} %get-tuple-element.13, f32[]{:T(128)} %get-tuple-element.12), channel_id=1, replica_groups=mesh['gx'=8,'gy'=4] {'gx','gy'}, use_global_device_ids=true, to_apply=%region_25.0 | all-reduce | flops 2 | bytes 16 | tf_op jit(solution)/shard_map/psum | solution.py:77
  482.4 4.5 collective-permute-start.43
  489.1 42.6 %all-reduce.4 = (f32[]{:T(128)}, f32[]{:T(128)}) all-reduce(f32[]{:T(128)} %get-tuple-element.11, f32[]{:T(128)} %get-tuple-element.10), channel_id=1, replica_groups=mesh['gx'=8,'gy'=4] {'gx','gy'}, use_global_device_ids=true, to_apply=%region_29.0 | all-reduce | flops 2 | bytes 16 | tf_op jit(solution)/shard_map/psum | solution.py:77
  544.5 4.5 collective-permute-start.47
  551.2 41.8 %all-reduce.3 = (f32[]{:T(128)}, f32[]{:T(128)}) all-reduce(f32[]{:T(128)} %get-tuple-element.9, f32[]{:T(128)} %get-tuple-element.8), channel_id=1, replica_groups=mesh['gx'=8,'gy'=4] {'gx','gy'}, use_global_device_ids=true, to_apply=%region_33.0 | all-reduce | flops 2 | bytes 16 | tf_op jit(solution)/shard_map/psum | solution.py:77
  620.5 4.5 collective-permute-start.55
  627.1 42.8 %all-reduce.2 = (f32[]{:T(128)}, f32[]{:T(128)}) all-reduce(f32[]{:T(128)} %get-tuple-element.7, f32[]{:T(128)} %get-tuple-element.6), channel_id=1, replica_groups=mesh['gx'=8,'gy'=4] {'gx','gy'}, use_global_device_ids=true, to_apply=%region_37.0 | all-reduce | flops 2 | bytes 16 | tf_op jit(solution)/shard_map/psum | solution.py:77
  679.5 4.5 collective-permute-start.59
  686.3 42.5 %all-reduce.1 = (f32[]{:T(128)}, f32[]{:T(128)}) all-reduce(f32[]{:T(128)} %get-tuple-element.5, f32[]{:T(128)} %get-tuple-element.4), channel_id=1, replica_groups=mesh['gx'=8,'gy'=4] {'gx','gy'}, use_global_device_ids=true, to_apply=%region_41.0 | all-reduce | flops 2 | bytes 16 | tf_op jit(solution)/shard_map/psum | solution.py:77
  741.6 4.5 collective-permute-start.63
  748.2 41.8 %all-reduce = (f32[]{:T(128)}, f32[]{:T(128)}) all-reduce(f32[]{:T(128)} %get-tuple-element.3, f32[]{:T(128)} %get-tuple-element.2), channel_id=1, replica_groups=mesh['gx'=8,'gy'=4] {'gx','gy'}, use_global_device_ids=true, to_apply=%region_45.0 | all-reduce | flops 2 | bytes 16 | tf_op jit(solution)/shard_map/psum | solution.py:77
  (190 shorter events, 191.0 us)
Async XLA Ops:
  26.6 5.8 collective-permute-start.6
  27.9 5.9 collective-permute-start.7
  85.6 5.8 collective-permute-start.10
  86.9 5.9 collective-permute-start.11
  147.8 5.8 collective-permute-start.14
  149.1 5.9 collective-permute-start.15
  224.3 5.8 collective-permute-start.22
  225.6 5.9 collective-permute-start.23
  283.1 5.8 collective-permute-start.26
  284.4 5.9 collective-permute-start.27
  345.2 5.8 collective-permute-start.30
  346.5 5.9 collective-permute-start.31
  422.1 5.8 collective-permute-start.38
  423.4 5.9 collective-permute-start.39
  481.1 5.8 collective-permute-start.42
  482.4 5.9 collective-permute-start.43
  543.2 5.8 collective-permute-start.46
  544.5 5.9 collective-permute-start.47
  619.2 5.8 collective-permute-start.54
  620.5 5.9 collective-permute-start.55
  678.3 5.8 collective-permute-start.58
  679.5 5.9 collective-permute-start.59
  740.3 5.8 collective-permute-start.62
  741.6 5.9 collective-permute-start.63
  (45 other events, 230.0 us)
where the time goes:
time: 799 us; the launch traced here: 795 us
  blocking collectives  508 us (64%)
  starting transfers between devices  135 us (17%)
  waiting for transfers between devices  95.6 us (12%)
  between operations  40.8 us (5%)
  other arithmetic  13.3 us (2%)
    psum x12, blocking collectives, paired(): lax.psum((jnp.sum(resid * resid), jnp.sum(resid * image)), ('gx', 'gy'))  508 us
    ppermute x32, starting transfers between devices, padded_2(): lax.ppermute(tail, axis, [(i, (i + 1) % count) for i in range(ends)])  93.9 us
    ppermute x32, waiting for transfers between devices, padded_2(): lax.ppermute(head, axis, [((i + 1) % count, i) for i in range(ends)])  78.5 us
    ppermute x32, starting transfers between devices, padded_2(): lax.ppermute(head, axis, [((i + 1) % count, i) for i in range(ends)])  41.2 us
    ppermute x32, waiting for transfers between devices, padded_2(): lax.ppermute(tail, axis, [(i, (i + 1) % count) for i in range(ends)])  17.1 us
  transfers between devices with their start and end apart: 64, of which 36 were waited for; matrix products, arithmetic and copies ran while one was open for 0% of the time, Pallas kernels for 0%

commit v1 on v0

--- a/solution.py
+++ b/solution.py
@@ -74,7 +74,7 @@
 
 
 def paired(resid, image):
-    return lax.psum((jnp.sum(resid * resid), jnp.sum(resid * image)), ("gx", "gy"))
+    return lax.psum(lax.psum((jnp.sum(resid * resid), jnp.sum(resid * image)), "gy"), "gx")
 
 
 def solve(rhs, diagonal):

time: 799 us -> 587 us (0.73)
  blocking collectives: 508 us -> 296 us
    psum x12 -> x24, blocking collectives: 508 us -> 296 us  [the longest x12 157 us: paired(): lax.psum(lax.psum((jnp.sum(resid * resid), jnp.sum(resid * image)), 'gy')...]
where the time goes in v1:
time: 587 us; the launch traced here: 582 us
  blocking collectives  296 us (50%)
  starting transfers between devices  140 us (24%)
  waiting for transfers between devices  91.2 us (16%)
  between operations  40.5 us (7%)
  other arithmetic  13.4 us (2%)
    psum x12, blocking collectives, paired(): lax.psum(lax.psum((jnp.sum(resid * resid), jnp.sum(resid * image)), 'gy')...  157 us
    psum x12, blocking collectives, paired(): lax.psum((jnp.sum(resid * resid), jnp.sum(resid * image)), 'gy')  138 us
    ppermute x32, starting transfers between devices, padded_2(): lax.ppermute(tail, axis, [(i, (i + 1) % count) for i in range(ends)])  98.9 us
    ppermute x32, waiting for transfers between devices, padded_2(): lax.ppermute(head, axis, [((i + 1) % count, i) for i in range(ends)])  74 us
    ppermute x32, starting transfers between devices, padded_2(): lax.ppermute(head, axis, [((i + 1) % count, i) for i in range(ends)])  41.2 us
    ppermute x32, waiting for transfers between devices, padded_2(): lax.ppermute(tail, axis, [(i, (i + 1) % count) for i in range(ends)])  17.1 us
  transfers between devices with their start and end apart: 64, of which 36 were waited for; matrix products, arithmetic and copies ran while one was open for 0% of the time, Pallas kernels for 0%

profile of v1, /device:TPU:0, one launch (start us, length us, event | category | flops | bytes accessed | tf_op | source)
XLA Modules:
  0.0 582.4 jit_solution(13555412365259933945)
XLA Ops:
  34.6 13.3 %all-reduce.23 = (f32[]{:T(128)}, f32[]{:T(128)}) all-reduce(f32[]{:T(128)} %get-tuple-element.25, f32[]{:T(128)} %get-tuple-element.24), channel_id=1, replica_groups=mesh['gx'=8,'gy'=4] {'gy'}, use_global_device_ids=true, to_apply=%region_1.0 | all-reduce | flops 2 | bytes 16 | tf_op jit(solution)/shard_map/psum | solution.py:77
  47.9 12.6 %all-reduce.11 = (f32[]{:T(128)}, f32[]{:T(128)}) all-reduce(f32[]{:T(128)} %get-tuple-element.72, f32[]{:T(128)} %get-tuple-element.73), channel_id=1, replica_groups=mesh['gx'=8,'gy'=4] {'gx'}, use_global_device_ids=true, to_apply=%region_2.0 | all-reduce | flops 2 | bytes 16 | tf_op jit(solution)/shard_map/psum | solution.py:77
  76.2 11.4 %all-reduce.22 = (f32[]{:T(128)}, f32[]{:T(128)}) all-reduce(f32[]{:T(128)} %get-tuple-element.23, f32[]{:T(128)} %get-tuple-element.22), channel_id=1, replica_groups=mesh['gx'=8,'gy'=4] {'gy'}, use_global_device_ids=true, to_apply=%region_7.0 | all-reduce | flops 2 | bytes 16 | tf_op jit(solution)/shard_map/psum | solution.py:77
  87.6 13.3 %all-reduce.10 = (f32[]{:T(128)}, f32[]{:T(128)}) all-reduce(f32[]{:T(128)} %get-tuple-element.70, f32[]{:T(128)} %get-tuple-element.71), channel_id=1, replica_groups=mesh['gx'=8,'gy'=4] {'gx'}, use_global_device_ids=true, to_apply=%region_8.0 | all-reduce | flops 2 | bytes 16 | tf_op jit(solution)/shard_map/psum | solution.py:77
  120.5 11.3 %all-reduce.21 = (f32[]{:T(128)}, f32[]{:T(128)}) all-reduce(f32[]{:T(128)} %get-tuple-element.21, f32[]{:T(128)} %get-tuple-element.20), channel_id=1, replica_groups=mesh['gx'=8,'gy'=4] {'gy'}, use_global_device_ids=true, to_apply=%region_13.0 | all-reduce | flops 2 | bytes 16 | tf_op jit(solution)/shard_map/psum | solution.py:77
  131.8 13.3 %all-reduce.9 = (f32[]{:T(128)}, f32[]{:T(128)}) all-reduce(f32[]{:T(128)} %get-tuple-element.68, f32[]{:T(128)} %get-tuple-element.69), channel_id=1, replica_groups=mesh['gx'=8,'gy'=4] {'gx'}, use_global_device_ids=true, to_apply=%region_14.0 | all-reduce | flops 2 | bytes 16 | tf_op jit(solution)/shard_map/psum | solution.py:77
  179.6 11.4 %all-reduce.20 = (f32[]{:T(128)}, f32[]{:T(128)}) all-reduce(f32[]{:T(128)} %get-tuple-element.19, f32[]{:T(128)} %get-tuple-element.18), channel_id=1, replica_groups=mesh['gx'=8,'gy'=4] {'gy'}, use_global_device_ids=true, to_apply=%region_19.0 | all-reduce | flops 2 | bytes 16 | tf_op jit(solution)/shard_map/psum | solution.py:77
  191.0 12.8 %all-reduce.8 = (f32[]{:T(128)}, f32[]{:T(128)}) all-reduce(f32[]{:T(128)} %get-tuple-element.66, f32[]{:T(128)} %get-tuple-element.67), channel_id=1, replica_groups=mesh['gx'=8,'gy'=4] {'gx'}, use_global_device_ids=true, to_apply=%region_20.0 | all-reduce | flops 2 | bytes 16 | tf_op jit(solution)/shard_map/psum | solution.py:77
  220.1 11.4 %all-reduce.19 = (f32[]{:T(128)}, f32[]{:T(128)}) all-reduce(f32[]{:T(128)} %get-tuple-element.17, f32[]{:T(128)} %get-tuple-element.16), channel_id=1, replica_groups=mesh['gx'=8,'gy'=4] {'gy'}, use_global_device_ids=true, to_apply=%region_25.0 | all-reduce | flops 2 | bytes 16 | tf_op jit(solution)/shard_map/psum | solution.py:77
  231.4 13.3 %all-reduce.7 = (f32[]{:T(128)}, f32[]{:T(128)}) all-reduce(f32[]{:T(128)} %get-tuple-element.64, f32[]{:T(128)} %get-tuple-element.65), channel_id=1, replica_groups=mesh['gx'=8,'gy'=4] {'gx'}, use_global_device_ids=true, to_apply=%region_26.0 | all-reduce | flops 2 | bytes 16 | tf_op jit(solution)/shard_map/psum | solution.py:77
  264.4 11.3 %all-reduce.18 = (f32[]{:T(128)}, f32[]{:T(128)}) all-reduce(f32[]{:T(128)} %get-tuple-element.15, f32[]{:T(128)} %get-tuple-element.14), channel_id=1, replica_groups=mesh['gx'=8,'gy'=4] {'gy'}, use_global_device_ids=true, to_apply=%region_31.0 | all-reduce | flops 2 | bytes 16 | tf_op jit(solution)/shard_map/psum | solution.py:77
  275.7 13.3 %all-reduce.6 = (f32[]{:T(128)}, f32[]{:T(128)}) all-reduce(f32[]{:T(128)} %get-tuple-element.62, f32[]{:T(128)} %get-tuple-element.63), channel_id=1, replica_groups=mesh['gx'=8,'gy'=4] {'gx'}, use_global_device_ids=true, to_apply=%region_32.0 | all-reduce | flops 2 | bytes 16 | tf_op jit(solution)/shard_map/psum | solution.py:77
  324.6 11.4 %all-reduce.17 = (f32[]{:T(128)}, f32[]{:T(128)}) all-reduce(f32[]{:T(128)} %get-tuple-element.13, f32[]{:T(128)} %get-tuple-element.12), channel_id=1, replica_groups=mesh['gx'=8,'gy'=4] {'gy'}, use_global_device_ids=true, to_apply=%region_37.0 | all-reduce | flops 2 | bytes 16 | tf_op jit(solution)/shard_map/psum | solution.py:77
  335.9 12.9 %all-reduce.5 = (f32[]{:T(128)}, f32[]{:T(128)}) all-reduce(f32[]{:T(128)} %get-tuple-element.60, f32[]{:T(128)} %get-tuple-element.61), channel_id=1, replica_groups=mesh['gx'=8,'gy'=4] {'gx'}, use_global_device_ids=true, to_apply=%region_38.0 | all-reduce | flops 2 | bytes 16 | tf_op jit(solution)/shard_map/psum | solution.py:77
  365.1 11.4 %all-reduce.16 = (f32[]{:T(128)}, f32[]{:T(128)}) all-reduce(f32[]{:T(128)} %get-tuple-element.11, f32[]{:T(128)} %get-tuple-element.10), channel_id=1, replica_groups=mesh['gx'=8,'gy'=4] {'gy'}, use_global_device_ids=true, to_apply=%region_43.0 | all-reduce | flops 2 | bytes 16 | tf_op jit(solution)/shard_map/psum | solution.py:77
  376.5 13.3 %all-reduce.4 = (f32[]{:T(128)}, f32[]{:T(128)}) all-reduce(f32[]{:T(128)} %get-tuple-element.58, f32[]{:T(128)} %get-tuple-element.59), channel_id=1, replica_groups=mesh['gx'=8,'gy'=4] {'gx'}, use_global_device_ids=true, to_apply=%region_44.0 | all-reduce | flops 2 | bytes 16 | tf_op jit(solution)/shard_map/psum | solution.py:77
  409.2 11.4 %all-reduce.15 = (f32[]{:T(128)}, f32[]{:T(128)}) all-reduce(f32[]{:T(128)} %get-tuple-element.9, f32[]{:T(128)} %get-tuple-element.8), channel_id=1, replica_groups=mesh['gx'=8,'gy'=4] {'gy'}, use_global_device_ids=true, to_apply=%region_49.0 | all-reduce | flops 2 | bytes 16 | tf_op jit(solution)/shard_map/psum | solution.py:77
  420.6 13.3 %all-reduce.3 = (f32[]{:T(128)}, f32[]{:T(128)}) all-reduce(f32[]{:T(128)} %get-tuple-element.56, f32[]{:T(128)} %get-tuple-element.57), channel_id=1, replica_groups=mesh['gx'=8,'gy'=4] {'gx'}, use_global_device_ids=true, to_apply=%region_50.0 | all-reduce | flops 2 | bytes 16 | tf_op jit(solution)/shard_map/psum | solution.py:77
  468.6 11.4 %all-reduce.14 = (f32[]{:T(128)}, f32[]{:T(128)}) all-reduce(f32[]{:T(128)} %get-tuple-element.7, f32[]{:T(128)} %get-tuple-element.6), channel_id=1, replica_groups=mesh['gx'=8,'gy'=4] {'gy'}, use_global_device_ids=true, to_apply=%region_55.0 | all-reduce | flops 2 | bytes 16 | tf_op jit(solution)/shard_map/psum | solution.py:77
  480.0 12.9 %all-reduce.2 = (f32[]{:T(128)}, f32[]{:T(128)}) all-reduce(f32[]{:T(128)} %get-tuple-element.54, f32[]{:T(128)} %get-tuple-element.55), channel_id=1, replica_groups=mesh['gx'=8,'gy'=4] {'gx'}, use_global_device_ids=true, to_apply=%region_56.0 | all-reduce | flops 2 | bytes 16 | tf_op jit(solution)/shard_map/psum | solution.py:77
  509.2 11.4 %all-reduce.13 = (f32[]{:T(128)}, f32[]{:T(128)}) all-reduce(f32[]{:T(128)} %get-tuple-element.5, f32[]{:T(128)} %get-tuple-element.4), channel_id=1, replica_groups=mesh['gx'=8,'gy'=4] {'gy'}, use_global_device_ids=true, to_apply=%region_61.0 | all-reduce | flops 2 | bytes 16 | tf_op jit(solution)/shard_map/psum | solution.py:77
  520.6 13.3 %all-reduce.1 = (f32[]{:T(128)}, f32[]{:T(128)}) all-reduce(f32[]{:T(128)} %get-tuple-element.52, f32[]{:T(128)} %get-tuple-element.53), channel_id=1, replica_groups=mesh['gx'=8,'gy'=4] {'gx'}, use_global_device_ids=true, to_apply=%region_62.0 | all-reduce | flops 2 | bytes 16 | tf_op jit(solution)/shard_map/psum | solution.py:77
  553.3 11.4 %all-reduce.12 = (f32[]{:T(128)}, f32[]{:T(128)}) all-reduce(f32[]{:T(128)} %get-tuple-element.3, f32[]{:T(128)} %get-tuple-element.2), channel_id=1, replica_groups=mesh['gx'=8,'gy'=4] {'gy'}, use_global_device_ids=true, to_apply=%region_67.0 | all-reduce | flops 2 | bytes 16 | tf_op jit(solution)/shard_map/psum | solution.py:77
  564.7 13.3 %all-reduce = (f32[]{:T(128)}, f32[]{:T(128)}) all-reduce(f32[]{:T(128)} %get-tuple-element.50, f32[]{:T(128)} %get-tuple-element.51), channel_id=1, replica_groups=mesh['gx'=8,'gy'=4] {'gx'}, use_global_device_ids=true, to_apply=%region_68.0 | all-reduce | flops 2 | bytes 16 | tf_op jit(solution)/shard_map/psum | solution.py:77
  (202 shorter events, 246.3 us)
Async XLA Ops:
  26.6 5.8 %collective-permute-start.6 = (f32[18,1]{1,0:T(8,128)S(1)}, f32[18,1]{1,0:T(8,128)S(1)}, u32[]{:S(2)}, u32[]{:S(2)}) collective-permute-start(f32[18,1]{1,0:T(8,128)S(1)} %get-tuple-element.114), channel_id=1, source_target_pairs={{1,0},{2,1},{3,2},{5,4},{6,5},{7,6},{9,8},{10,9},{11,10},{13,12},{... | collective-permute-start | bytes 224 | tf_op jit(solution)/shard_map/ppermute | solution.py:22
  27.9 5.9 %collective-permute-start.7 = (f32[18,1]{1,0:T(8,128)S(1)}, f32[18,1]{1,0:T(8,128)S(1)}, u32[]{:S(2)}, u32[]{:S(2)}) collective-permute-start(f32[18,1]{1,0:T(8,128)S(1)} %get-tuple-element.115), channel_id=1, source_target_pairs={{0,1},{1,2},{2,3},{4,5},{5,6},{6,7},{8,9},{9,10},{10,11},{12,13},{... | collective-permute-start | bytes 224 | tf_op jit(solution)/shard_map/ppermute | solution.py:20
  68.2 5.8 %collective-permute-start.10 = (f32[18,1]{1,0:T(8,128)S(1)}, f32[18,1]{1,0:T(8,128)S(1)}, u32[]{:S(2)}, u32[]{:S(2)}) collective-permute-start(f32[18,1]{1,0:T(8,128)S(1)} %get-tuple-element.112), channel_id=1, source_target_pairs={{1,0},{2,1},{3,2},{5,4},{6,5},{7,6},{9,8},{10,9},{11,10},{13,12},{... | collective-permute-start | bytes 224 | tf_op jit(solution)/shard_map/ppermute | solution.py:22
  69.5 5.9 %collective-permute-start.11 = (f32[18,1]{1,0:T(8,128)S(1)}, f32[18,1]{1,0:T(8,128)S(1)}, u32[]{:S(2)}, u32[]{:S(2)}) collective-permute-start(f32[18,1]{1,0:T(8,128)S(1)} %get-tuple-element.113), channel_id=1, source_target_pairs={{0,1},{1,2},{2,3},{4,5},{5,6},{6,7},{8,9},{9,10},{10,11},{12,13},{... | collective-permute-start | bytes 224 | tf_op jit(solution)/shard_map/ppermute | solution.py:20
  112.6 5.8 %collective-permute-start.14 = (f32[18,1]{1,0:T(8,128)S(1)}, f32[18,1]{1,0:T(8,128)S(1)}, u32[]{:S(2)}, u32[]{:S(2)}) collective-permute-start(f32[18,1]{1,0:T(8,128)S(1)} %get-tuple-element.110), channel_id=1, source_target_pairs={{1,0},{2,1},{3,2},{5,4},{6,5},{7,6},{9,8},{10,9},{11,10},{13,12},{... | collective-permute-start | bytes 224 | tf_op jit(solution)/shard_map/ppermute | solution.py:22
  113.9 5.9 %collective-permute-start.15 = (f32[18,1]{1,0:T(8,128)S(1)}, f32[18,1]{1,0:T(8,128)S(1)}, u32[]{:S(2)}, u32[]{:S(2)}) collective-permute-start(f32[18,1]{1,0:T(8,128)S(1)} %get-tuple-element.111), channel_id=1, source_target_pairs={{0,1},{1,2},{2,3},{4,5},{5,6},{6,7},{8,9},{9,10},{10,11},{12,13},{... | collective-permute-start | bytes 224 | tf_op jit(solution)/shard_map/ppermute | solution.py:20
  171.6 5.8 %collective-permute-start.22 = (f32[18,1]{1,0:T(8,128)S(1)}, f32[18,1]{1,0:T(8,128)S(1)}, u32[]{:S(2)}, u32[]{:S(2)}) collective-permute-start(f32[18,1]{1,0:T(8,128)S(1)} %get-tuple-element.106), channel_id=1, source_target_pairs={{1,0},{2,1},{3,2},{5,4},{6,5},{7,6},{9,8},{10,9},{11,10},{13,12},{... | collective-permute-start | bytes 224 | tf_op jit(solution)/shard_map/ppermute | solution.py:22
  172.9 5.9 %collective-permute-start.23 = (f32[18,1]{1,0:T(8,128)S(1)}, f32[18,1]{1,0:T(8,128)S(1)}, u32[]{:S(2)}, u32[]{:S(2)}) collective-permute-start(f32[18,1]{1,0:T(8,128)S(1)} %get-tuple-element.107), channel_id=1, source_target_pairs={{0,1},{1,2},{2,3},{4,5},{5,6},{6,7},{8,9},{9,10},{10,11},{12,13},{... | collective-permute-start | bytes 224 | tf_op jit(solution)/shard_map/ppermute | solution.py:20
  212.1 5.8 %collective-permute-start.26 = (f32[18,1]{1,0:T(8,128)S(1)}, f32[18,1]{1,0:T(8,128)S(1)}, u32[]{:S(2)}, u32[]{:S(2)}) collective-permute-start(f32[18,1]{1,0:T(8,128)S(1)} %get-tuple-element.104), channel_id=1, source_target_pairs={{1,0},{2,1},{3,2},{5,4},{6,5},{7,6},{9,8},{10,9},{11,10},{13,12},{... | collective-permute-start | bytes 224 | tf_op jit(solution)/shard_map/ppermute | solution.py:22
  213.4 5.9 %collective-permute-start.27 = (f32[18,1]{1,0:T(8,128)S(1)}, f32[18,1]{1,0:T(8,128)S(1)}, u32[]{:S(2)}, u32[]{:S(2)}) collective-permute-start(f32[18,1]{1,0:T(8,128)S(1)} %get-tuple-element.105), channel_id=1, source_target_pairs={{0,1},{1,2},{2,3},{4,5},{5,6},{6,7},{8,9},{9,10},{10,11},{12,13},{... | collective-permute-start | bytes 224 | tf_op jit(solution)/shard_map/ppermute | solution.py:20
  256.4 5.8 %collective-permute-start.30 = (f32[18,1]{1,0:T(8,128)S(1)}, f32[18,1]{1,0:T(8,128)S(1)}, u32[]{:S(2)}, u32[]{:S(2)}) collective-permute-start(f32[18,1]{1,0:T(8,128)S(1)} %get-tuple-element.102), channel_id=1, source_target_pairs={{1,0},{2,1},{3,2},{5,4},{6,5},{7,6},{9,8},{10,9},{11,10},{13,12},{... | collective-permute-start | bytes 224 | tf_op jit(solution)/shard_map/ppermute | solution.py:22
  257.7 5.9 %collective-permute-start.31 = (f32[18,1]{1,0:T(8,128)S(1)}, f32[18,1]{1,0:T(8,128)S(1)}, u32[]{:S(2)}, u32[]{:S(2)}) collective-permute-start(f32[18,1]{1,0:T(8,128)S(1)} %get-tuple-element.103), channel_id=1, source_target_pairs={{0,1},{1,2},{2,3},{4,5},{5,6},{6,7},{8,9},{9,10},{10,11},{12,13},{... | collective-permute-start | bytes 224 | tf_op jit(solution)/shard_map/ppermute | solution.py:20
  316.5 5.8 %collective-permute-start.38 = (f32[18,1]{1,0:T(8,128)S(1)}, f32[18,1]{1,0:T(8,128)S(1)}, u32[]{:S(2)}, u32[]{:S(2)}) collective-permute-start(f32[18,1]{1,0:T(8,128)S(1)} %get-tuple-element.100), channel_id=1, source_target_pairs={{1,0},{2,1},{3,2},{5,4},{6,5},{7,6},{9,8},{10,9},{11,10},{13,12},{... | collective-permute-start | bytes 224 | tf_op jit(solution)/shard_map/ppermute | solution.py:22
  317.8 5.9 %collective-permute-start.39 = (f32[18,1]{1,0:T(8,128)S(1)}, f32[18,1]{1,0:T(8,128)S(1)}, u32[]{:S(2)}, u32[]{:S(2)}) collective-permute-start(f32[18,1]{1,0:T(8,128)S(1)} %get-tuple-element.101), channel_id=1, source_target_pairs={{0,1},{1,2},{2,3},{4,5},{5,6},{6,7},{8,9},{9,10},{10,11},{12,13},{... | collective-permute-start | bytes 224 | tf_op jit(solution)/shard_map/ppermute | solution.py:20
  357.2 5.8 %collective-permute-start.42 = (f32[18,1]{1,0:T(8,128)S(1)}, f32[18,1]{1,0:T(8,128)S(1)}, u32[]{:S(2)}, u32[]{:S(2)}) collective-permute-start(f32[18,1]{1,0:T(8,128)S(1)} %get-tuple-element.98), channel_id=1, source_target_pairs={{1,0},{2,1},{3,2},{5,4},{6,5},{7,6},{9,8},{10,9},{11,10},{13,12},{... | collective-permute-start | bytes 224 | tf_op jit(solution)/shard_map/ppermute | solution.py:22
  358.5 5.9 %collective-permute-start.43 = (f32[18,1]{1,0:T(8,128)S(1)}, f32[18,1]{1,0:T(8,128)S(1)}, u32[]{:S(2)}, u32[]{:S(2)}) collective-permute-start(f32[18,1]{1,0:T(8,128)S(1)} %get-tuple-element.99), channel_id=1, source_target_pairs={{0,1},{1,2},{2,3},{4,5},{5,6},{6,7},{8,9},{9,10},{10,11},{12,13},{... | collective-permute-start | bytes 224 | tf_op jit(solution)/shard_map/ppermute | solution.py:20
  401.3 5.8 %collective-permute-start.46 = (f32[18,1]{1,0:T(8,128)S(1)}, f32[18,1]{1,0:T(8,128)S(1)}, u32[]{:S(2)}, u32[]{:S(2)}) collective-permute-start(f32[18,1]{1,0:T(8,128)S(1)} %get-tuple-element.96), channel_id=1, source_target_pairs={{1,0},{2,1},{3,2},{5,4},{6,5},{7,6},{9,8},{10,9},{11,10},{13,12},{... | collective-permute-start | bytes 224 | tf_op jit(solution)/shard_map/ppermute | solution.py:22
  402.6 5.9 %collective-permute-start.47 = (f32[18,1]{1,0:T(8,128)S(1)}, f32[18,1]{1,0:T(8,128)S(1)}, u32[]{:S(2)}, u32[]{:S(2)}) collective-permute-start(f32[18,1]{1,0:T(8,128)S(1)} %get-tuple-element.97), channel_id=1, source_target_pairs={{0,1},{1,2},{2,3},{4,5},{5,6},{6,7},{8,9},{9,10},{10,11},{12,13},{... | collective-permute-start | bytes 224 | tf_op jit(solution)/shard_map/ppermute | solution.py:20
  460.6 5.8 %collective-permute-start.54 = (f32[18,1]{1,0:T(8,128)S(1)}, f32[18,1]{1,0:T(8,128)S(1)}, u32[]{:S(2)}, u32[]{:S(2)}) collective-permute-start(f32[18,1]{1,0:T(8,128)S(1)} %get-tuple-element.94), channel_id=1, source_target_pairs={{1,0},{2,1},{3,2},{5,4},{6,5},{7,6},{9,8},{10,9},{11,10},{13,12},{... | collective-permute-start | bytes 224 | tf_op jit(solution)/shard_map/ppermute | solution.py:22
  461.9 5.9 %collective-permute-start.55 = (f32[18,1]{1,0:T(8,128)S(1)}, f32[18,1]{1,0:T(8,128)S(1)}, u32[]{:S(2)}, u32[]{:S(2)}) collective-permute-start(f32[18,1]{1,0:T(8,128)S(1)} %get-tuple-element.95), channel_id=1, source_target_pairs={{0,1},{1,2},{2,3},{4,5},{5,6},{6,7},{8,9},{9,10},{10,11},{12,13},{... | collective-permute-start | bytes 224 | tf_op jit(solution)/shard_map/ppermute | solution.py:20
  501.3 5.8 %collective-permute-start.58 = (f32[18,1]{1,0:T(8,128)S(1)}, f32[18,1]{1,0:T(8,128)S(1)}, u32[]{:S(2)}, u32[]{:S(2)}) collective-permute-start(f32[18,1]{1,0:T(8,128)S(1)} %get-tuple-element.92), channel_id=1, source_target_pairs={{1,0},{2,1},{3,2},{5,4},{6,5},{7,6},{9,8},{10,9},{11,10},{13,12},{... | collective-permute-start | bytes 224 | tf_op jit(solution)/shard_map/ppermute | solution.py:22
  502.5 5.9 %collective-permute-start.59 = (f32[18,1]{1,0:T(8,128)S(1)}, f32[18,1]{1,0:T(8,128)S(1)}, u32[]{:S(2)}, u32[]{:S(2)}) collective-permute-start(f32[18,1]{1,0:T(8,128)S(1)} %get-tuple-element.93), channel_id=1, source_target_pairs={{0,1},{1,2},{2,3},{4,5},{5,6},{6,7},{8,9},{9,10},{10,11},{12,13},{... | collective-permute-start | bytes 224 | tf_op jit(solution)/shard_map/ppermute | solution.py:20
  545.4 5.8 %collective-permute-start.62 = (f32[18,1]{1,0:T(8,128)S(1)}, f32[18,1]{1,0:T(8,128)S(1)}, u32[]{:S(2)}, u32[]{:S(2)}) collective-permute-start(f32[18,1]{1,0:T(8,128)S(1)} %get-tuple-element.90), channel_id=1, source_target_pairs={{1,0},{2,1},{3,2},{5,4},{6,5},{7,6},{9,8},{10,9},{11,10},{13,12},{... | collective-permute-start | bytes 224 | tf_op jit(solution)/shard_map/ppermute | solution.py:22
  546.6 5.9 %collective-permute-start.63 = (f32[18,1]{1,0:T(8,128)S(1)}, f32[18,1]{1,0:T(8,128)S(1)}, u32[]{:S(2)}, u32[]{:S(2)}) collective-permute-start(f32[18,1]{1,0:T(8,128)S(1)} %get-tuple-element.91), channel_id=1, source_target_pairs={{0,1},{1,2},{2,3},{4,5},{5,6},{6,7},{8,9},{9,10},{10,11},{12,13},{... | collective-permute-start | bytes 224 | tf_op jit(solution)/shard_map/ppermute | solution.py:20
  (45 other events, 228.2 us)
